TPU v7x, 32 devices: a whole 2x2x4 slice. The times are simulated.
32 devices in a mesh: groups: 2 (over y), axial: 16 (over z, x, core).
Axes of the slice: x: 2, y: 2, z: 4, core: 2. Of those that a mesh axis runs over, the one named last changes fastest.
Arguments:
- pair_rep: bfloat16 [192, 96, 128], P(('groups', 'axial')), parts along dimension 0, may hold values from -6 to 6
- norm_out: float32 [128], replicated, may hold values from 0.5 to 1.5
- proj_out: bfloat16 [128, 512], replicated, may hold values from -0.5 to 0.5
- gate_out: bfloat16 [128, 128], replicated, may hold values from -0.5 to 0.5
- mid_out: float32 [128], replicated, may hold values from 0.5 to 1.5
- final_out: bfloat16 [128, 128], replicated, may hold values from -0.5 to 0.5
- norm_in: float32 [128], replicated, may hold values from 0.5 to 1.5
- proj_in: bfloat16 [128, 512], replicated, may hold values from -0.5 to 0.5
- gate_in: bfloat16 [128, 128], replicated, may hold values from -0.5 to 0.5
- mid_in: float32 [128], replicated, may hold values from 0.5 to 1.5
- final_in: bfloat16 [128, 128], replicated, may hold values from -0.5 to 0.5
Outputs:
- updated: bfloat16 [192, 96, 128], P(('groups', 'axial')), parts along dimension 0
There are 2 independent parts, one for each index of `groups`. A program takes and returns all parts, laid end to end along the dimension named above; an argument that names none is the same for every part. Nothing has to cross between parts.
All inputs are finite; a program needn't handle non-finite values.
Results may differ from a plain program's by a relative error of at most 0.013.
Values may be sent and summed in bfloat16 or wider, within the bound.
A program may use at most 64 MiB of HBM per device.

v0:
```python
import jax
import jax.numpy as jnp
from jax import lax
from jax.sharding import PartitionSpec as P

EPS = 1e-05


def normalize(values, gain, axis):
    average = jnp.mean(values, axis=axis, keepdims=True)
    spread = jnp.mean(jnp.square(values - average), axis=axis, keepdims=True)
    return (values - average) * lax.rsqrt(spread + EPS) * gain


def channel_product(left_side, right_side, outgoing):
    formula = "kil,kjl->kij" if outgoing else "kli,klj->kij"
    got_left, got_right = (
        lax.all_to_all(left_side, "axial", split_axis=0, concat_axis=1, tiled=True),
        lax.all_to_all(right_side, "axial", split_axis=0, concat_axis=1, tiled=True),
    )
    return jnp.einsum(formula, got_left, got_right, preferred_element_type=jnp.float32)


def update(pair_rep, norm_gain, weights, gate_weight, mid_gain, final_weight, outgoing):
    normed = normalize(pair_rep.astype(jnp.float32), norm_gain, -1).astype(jnp.bfloat16)
    projected = jnp.einsum("rnc,ck->krn", normed, weights, preferred_element_type=jnp.float32)
    hidden = weights.shape[1] // 4
    left_side = (jax.nn.sigmoid(projected[hidden : 2 * hidden]) * projected[:hidden]).astype(
        jnp.bfloat16
    )
    right_side = (
        jax.nn.sigmoid(projected[3 * hidden :]) * projected[2 * hidden : 3 * hidden]
    ).astype(jnp.bfloat16)
    product = channel_product(left_side, right_side, outgoing)
    tri = lax.all_to_all(
        product.astype(jnp.bfloat16), "axial", split_axis=1, concat_axis=0, tiled=True
    )
    gating = jax.nn.sigmoid(
        jnp.einsum("rnc,ce->rne", normed, gate_weight, preferred_element_type=jnp.float32)
    )
    tri_normed = normalize(tri.astype(jnp.float32), mid_gain[:, None, None], 0).astype(jnp.bfloat16)
    result = jnp.einsum("krn,kc->rnc", tri_normed, final_weight, preferred_element_type=jnp.float32)
    return (pair_rep.astype(jnp.float32) + gating * result).astype(jnp.bfloat16)


def on_device(
    pair_rep,
    norm_out,
    proj_out,
    gate_out,
    mid_out,
    final_out,
    norm_in,
    proj_in,
    gate_in,
    mid_in,
    final_in,
):
    first = update(pair_rep, norm_out, proj_out, gate_out, mid_out, final_out, True)
    return update(first, norm_in, proj_in, gate_in, mid_in, final_in, False)


def solution(mesh):
    placed = (P(("groups", "axial"), None, None), P(), P(), P(), P(), P(), P(), P(), P(), P(), P())
    return jax.shard_map(
        on_device,
        mesh=mesh,
        in_specs=placed,
        out_specs=P(("groups", "axial"), None, None),
        check_vma=False,
    )
```

profile of v0, /device:TPU:0, one launch (start us, length us, event | category | flops | bytes accessed | tf_op | source)
XLA Modules:
  0.0 93.4 jit_solution(2439038225981949099)
XLA Ops:
  0.0 1.1 %convert_reduce_fusion = f32[6,96]{1,0:T(8,128)S(1)} fusion(bf16[6,96,128]{2,1,0:T(8,128)(2,1)} %param.11), kind=kLoop, calls=%fused_computation.20 | loop fusion | flops 146880 | bytes 149760 | tf_op jit(solution)/shard_map/reduce_sum | solution.py:10
  1.1 1.2 %fusion.19 = f32[6,96]{1,0:T(8,128)S(1)} fusion(bf16[6,96,128]{2,1,0:T(8,128)(2,1)} %param.11, f32[6,96]{1,0:T(8,128)S(1)} %broadcast_multiply_fusion.3), kind=kLoop, calls=%fused_computation.35 | loop fusion | flops 294336 | bytes 152064 | tf_op jit(solution)/shard_map/reduce_sum | solution.py:11
  2.3 1.3 %convolution_bitcast_fusion.1 = f32[512,6,96]{0,2,1:T(8,128)S(1)} fusion(bf16[128,512]{1,0:T(8,128)(2,1)S(1)} %copy-done, bf16[6,96,128]{2,1,0:T(8,128)(2,1)} %param.11, f32[128]{0:T(128)} %param.12, f32[6,96]{1,0:T(8,128)S(1)} %add_rsqrt_fusion.3, f32[6,96]{1,0:T(8,128)S(1)} %broadcast_multiply_fusion.3), kind=kOutput, calls=%fused_computation.1 | convolution fusion | flops 75866112 | bytes 1463296 | tf_op jit(solution)/shard_map/rnc,ck->krn/dot_general | solution.py:26
  3.6 0.2 fusion.34
  3.8 0.9 copy.39
  4.6 7.4 %all-to-all-start.1 = ((bf16[128,6,96]{2,1,0:T(8,128)(2,1)}), bf16[128,6,96]{2,1,0:T(8,128)(2,1)S(1)}, u32[]{:S(2)}, u32[]{:S(2)}) async-start(bf16[128,6,96]{2,1,0:T(8,128)(2,1)} %copy.39), calls=%async_computation.1 | async-start | bytes 524288 | tf_op jit(solution)/shard_map/all_to_all | solution.py:19
  12.0 0.9 copy.36
  12.9 9.1 %all-to-all-done.1 = bf16[128,6,96]{2,1,0:T(8,128)(2,1)S(1)} async-done(((bf16[128,6,96]{2,1,0:T(8,128)(2,1)}), bf16[128,6,96]{2,1,0:T(8,128)(2,1)S(1)}, u32[]{:S(2)}, u32[]{:S(2)}) %all-to-all-start.1) | async-done | bytes 147488 | tf_op jit(solution)/shard_map/all_to_all | solution.py:19
  22.1 3.5 %all-to-all-start = ((bf16[128,6,96]{2,1,0:T(8,128)(2,1)}), bf16[128,6,96]{2,1,0:T(8,128)(2,1)S(1)}, u32[]{:S(2)}, u32[]{:S(2)}) async-start(bf16[128,6,96]{2,1,0:T(8,128)(2,1)} %copy.36), calls=%async_computation | async-start | bytes 524288 | tf_op jit(solution)/shard_map/all_to_all | solution.py:18
  25.7 9.9 %all-to-all-done = bf16[128,6,96]{2,1,0:T(8,128)(2,1)S(1)} async-done(((bf16[128,6,96]{2,1,0:T(8,128)(2,1)}), bf16[128,6,96]{2,1,0:T(8,128)(2,1)S(1)}, u32[]{:S(2)}, u32[]{:S(2)}) %all-to-all-start) | async-done | bytes 147488 | tf_op jit(solution)/shard_map/all_to_all | solution.py:18
  35.6 0.2 convolution_convert_fusion.1
  35.9 0.7 copy.44
  36.6 3.7 %all-to-all-start.2 = ((bf16[8,96,96]{2,0,1:T(8,128)(2,1)}), bf16[8,96,96]{2,0,1:T(8,128)(2,1)S(1)}, u32[]{:S(2)}, u32[]{:S(2)}) async-start(bf16[8,96,96]{2,0,1:T(8,128)(2,1)} %copy.44), calls=%async_computation.2 | async-start | bytes 393216 | tf_op jit(solution)/shard_map/all_to_all | solution.py:35
  40.3 0.3 fusion.7
  40.7 8.5 %all-to-all-done.2 = bf16[8,96,96]{2,0,1:T(8,128)(2,1)S(1)} async-done(((bf16[8,96,96]{2,0,1:T(8,128)(2,1)}), bf16[8,96,96]{2,0,1:T(8,128)(2,1)S(1)}, u32[]{:S(2)}, u32[]{:S(2)}) %all-to-all-start.2) | async-done | bytes 147488 | tf_op jit(solution)/shard_map/all_to_all | solution.py:35
  49.3 0.1 multiply_reduce_fusion.1
  49.4 0.4 fusion.60
  49.8 0.3 multiply_reduce_fusion.2
  50.1 0.4 convolution_bitcast_fusion
  50.5 0.2 fusion.26
  50.7 0.9 copy.47
  51.6 3.5 %all-to-all-start.3 = ((bf16[128,6,96]{2,1,0:T(8,128)(2,1)}), bf16[128,6,96]{2,1,0:T(8,128)(2,1)S(1)}, u32[]{:S(2)}, u32[]{:S(2)}) async-start(bf16[128,6,96]{2,1,0:T(8,128)(2,1)} %copy.47), calls=%async_computation.3 | async-start | bytes 524288 | tf_op jit(solution)/shard_map/all_to_all | solution.py:18
  55.1 0.9 copy.50
  56.0 9.1 %all-to-all-done.3 = bf16[128,6,96]{2,1,0:T(8,128)(2,1)S(1)} async-done(((bf16[128,6,96]{2,1,0:T(8,128)(2,1)}), bf16[128,6,96]{2,1,0:T(8,128)(2,1)S(1)}, u32[]{:S(2)}, u32[]{:S(2)}) %all-to-all-start.3) | async-done | bytes 147488 | tf_op jit(solution)/shard_map/all_to_all | solution.py:18
  65.1 3.5 %all-to-all-start.4 = ((bf16[128,6,96]{2,1,0:T(8,128)(2,1)}), bf16[128,6,96]{2,1,0:T(8,128)(2,1)S(1)}, u32[]{:S(2)}, u32[]{:S(2)}) async-start(bf16[128,6,96]{2,1,0:T(8,128)(2,1)} %copy.50), calls=%async_computation.4 | async-start | bytes 524288 | tf_op jit(solution)/shard_map/all_to_all | solution.py:19
  68.7 9.9 %all-to-all-done.4 = bf16[128,6,96]{2,1,0:T(8,128)(2,1)S(1)} async-done(((bf16[128,6,96]{2,1,0:T(8,128)(2,1)}), bf16[128,6,96]{2,1,0:T(8,128)(2,1)S(1)}, u32[]{:S(2)}, u32[]{:S(2)}) %all-to-all-start.4) | async-done | bytes 147488 | tf_op jit(solution)/shard_map/all_to_all | solution.py:19
  78.6 0.3 convolution_convert_fusion
  78.9 0.7 copy.55
  79.6 3.7 %all-to-all-start.5 = ((bf16[8,96,96]{2,0,1:T(8,128)(2,1)}), bf16[8,96,96]{2,0,1:T(8,128)(2,1)S(1)}, u32[]{:S(2)}, u32[]{:S(2)}) async-start(bf16[8,96,96]{2,0,1:T(8,128)(2,1)} %copy.55), calls=%async_computation.5 | async-start | bytes 393216 | tf_op jit(solution)/shard_map/all_to_all | solution.py:35
  83.3 0.3 fusion.4
  83.7 8.6 %all-to-all-done.5 = bf16[8,96,96]{2,0,1:T(8,128)(2,1)S(1)} async-done(((bf16[8,96,96]{2,0,1:T(8,128)(2,1)}), bf16[8,96,96]{2,0,1:T(8,128)(2,1)S(1)}, u32[]{:S(2)}, u32[]{:S(2)}) %all-to-all-start.5) | async-done | bytes 147488 | tf_op jit(solution)/shard_map/all_to_all | solution.py:35
  92.4 1.0 %fusion.10 = bf16[6,96,128]{2,1,0:T(8,128)(2,1)} fusion(f32[6,96,128]{2,1,0:T(8,128)S(1)} %get-tuple-element.10, f32[6,96,128]{2,1,0:T(8,128)S(1)} %fusion.4, f32[128]{0:T(128)S(1)} %copy-done.6, f32[6,96]{1,0:T(8,128)S(1)} %add_rsqrt_fusion, f32[6,96]{1,0:T(8,128)S(1)} %broadcast_multiply_fusion, bf16[128,128]{1,0:T(8,128)(2,1)S(1)} %copy-done.4, ...), kind=kOutput, calls=%fused_computation.18 | convolution fusion | flops 19464192 | bytes 922624 | tf_op jit(solution)/shard_map/krn,kc->rnc/dot_general | solution.py:42
  (37 shorter events, 0.4 us)
Async XLA Ops:
  0.0 2.3 %copy-start = (bf16[128,512]{1,0:T(8,128)(2,1)S(1)}, bf16[128,512]{1,0:T(8,128)(2,1)}, u32[]{:S(2)}) copy-start(bf16[128,512]{1,0:T(8,128)(2,1)} %param.13) | copy-start | bytes 393220
  4.6 17.4 %all-to-all-start.1 = ((bf16[128,6,96]{2,1,0:T(8,128)(2,1)}), bf16[128,6,96]{2,1,0:T(8,128)(2,1)S(1)}, u32[]{:S(2)}, u32[]{:S(2)}) async-start(bf16[128,6,96]{2,1,0:T(8,128)(2,1)} %copy.39), calls=%async_computation.1 | async-start | bytes 524288 | tf_op jit(solution)/shard_map/all_to_all | solution.py:19
  22.1 13.5 %all-to-all-start = ((bf16[128,6,96]{2,1,0:T(8,128)(2,1)}), bf16[128,6,96]{2,1,0:T(8,128)(2,1)S(1)}, u32[]{:S(2)}, u32[]{:S(2)}) async-start(bf16[128,6,96]{2,1,0:T(8,128)(2,1)} %copy.36), calls=%async_computation | async-start | bytes 524288 | tf_op jit(solution)/shard_map/all_to_all | solution.py:18
  25.6 14.7 %copy-start.1 = (bf16[6,96,128]{2,1,0:T(8,128)(2,1)S(1)}, bf16[6,96,128]{2,1,0:T(8,128)(2,1)}, u32[]{:S(2)}) copy-start(bf16[6,96,128]{2,1,0:T(8,128)(2,1)} %param.11) | copy-start | bytes 442372
  25.6 14.7 %copy-start.7 = (f32[128]{0:T(128)S(1)}, f32[128]{0:T(128)}, u32[]{:S(2)}) copy-start(f32[128]{0:T(128)} %param.12) | copy-start | bytes 1540
  25.6 14.7 %copy-start.9 = (bf16[128,128]{1,0:T(8,128)(2,1)S(1)}, bf16[128,128]{1,0:T(8,128)(2,1)}, u32[]{:S(2)}) copy-start(bf16[128,128]{1,0:T(8,128)(2,1)} %param.14) | copy-start | bytes 98308
  36.6 12.8 %copy-start.3 = (bf16[128,128]{1,0:T(8,128)(2,1)S(1)}, bf16[128,128]{1,0:T(8,128)(2,1)}, u32[]{:S(2)}) copy-start(bf16[128,128]{1,0:T(8,128)(2,1)} %param.16) | copy-start | bytes 98308
  36.6 12.8 %copy-start.5 = (f32[128]{0:T(128)S(1)}, f32[128]{0:T(128)}, u32[]{:S(2)}) copy-start(f32[128]{0:T(128)} %param.15) | copy-start | bytes 1540
  36.6 12.6 %all-to-all-start.2 = ((bf16[8,96,96]{2,0,1:T(8,128)(2,1)}), bf16[8,96,96]{2,0,1:T(8,128)(2,1)S(1)}, u32[]{:S(2)}, u32[]{:S(2)}) async-start(bf16[8,96,96]{2,0,1:T(8,128)(2,1)} %copy.44), calls=%async_computation.2 | async-start | bytes 393216 | tf_op jit(solution)/shard_map/all_to_all | solution.py:35
  40.7 9.5 %copy-start.2 = (bf16[128,512]{1,0:T(8,128)(2,1)S(1)}, bf16[128,512]{1,0:T(8,128)(2,1)}, u32[]{:S(2)}) copy-start(bf16[128,512]{1,0:T(8,128)(2,1)} %param.18) | copy-start | bytes 393220
  40.7 9.5 %copy-start.8 = (f32[128]{0:T(128)S(1)}, f32[128]{0:T(128)}, u32[]{:S(2)}) copy-start(f32[128]{0:T(128)} %param.17) | copy-start | bytes 1540
  51.6 13.5 %all-to-all-start.3 = ((bf16[128,6,96]{2,1,0:T(8,128)(2,1)}), bf16[128,6,96]{2,1,0:T(8,128)(2,1)S(1)}, u32[]{:S(2)}, u32[]{:S(2)}) async-start(bf16[128,6,96]{2,1,0:T(8,128)(2,1)} %copy.47), calls=%async_computation.3 | async-start | bytes 524288 | tf_op jit(solution)/shard_map/all_to_all | solution.py:18
  65.1 13.5 %all-to-all-start.4 = ((bf16[128,6,96]{2,1,0:T(8,128)(2,1)}), bf16[128,6,96]{2,1,0:T(8,128)(2,1)S(1)}, u32[]{:S(2)}, u32[]{:S(2)}) async-start(bf16[128,6,96]{2,1,0:T(8,128)(2,1)} %copy.50), calls=%async_computation.4 | async-start | bytes 524288 | tf_op jit(solution)/shard_map/all_to_all | solution.py:19
  68.6 14.7 %copy-start.10 = (bf16[128,128]{1,0:T(8,128)(2,1)S(1)}, bf16[128,128]{1,0:T(8,128)(2,1)}, u32[]{:S(2)}) copy-start(bf16[128,128]{1,0:T(8,128)(2,1)} %param.19) | copy-start | bytes 98308
  79.6 12.8 %copy-start.4 = (bf16[128,128]{1,0:T(8,128)(2,1)S(1)}, bf16[128,128]{1,0:T(8,128)(2,1)}, u32[]{:S(2)}) copy-start(bf16[128,128]{1,0:T(8,128)(2,1)} %param.21) | copy-start | bytes 98308
  79.6 12.8 %copy-start.6 = (f32[128]{0:T(128)S(1)}, f32[128]{0:T(128)}, u32[]{:S(2)}) copy-start(f32[128]{0:T(128)} %param.20) | copy-start | bytes 1540
  79.6 12.6 %all-to-all-start.5 = ((bf16[8,96,96]{2,0,1:T(8,128)(2,1)}), bf16[8,96,96]{2,0,1:T(8,128)(2,1)S(1)}, u32[]{:S(2)}, u32[]{:S(2)}) async-start(bf16[8,96,96]{2,0,1:T(8,128)(2,1)} %copy.55), calls=%async_computation.5 | async-start | bytes 393216 | tf_op jit(solution)/shard_map/all_to_all | solution.py:35
where the time goes:
time: 94.3 us; the launch traced here: 93.4 us
  waiting for transfers between devices  55.1 us (58%)
  starting transfers between devices  25.3 us (27%)
  local copies, waits for them, and re-layouts  5.17 us (5%)
  matrix products  4.23 us (4%)
  other arithmetic  3.23 us (3%)
    all_to_all x2, waiting for transfers between devices, channel_product(): lax.all_to_all(right_side, 'axial', split_axis=0, concat_axis=1, tiled=True)  19.1 us
    all_to_all x2, waiting for transfers between devices, channel_product(): lax.all_to_all(left_side, 'axial', split_axis=0, concat_axis=1, tiled=True)  19 us
    all_to_all x2, waiting for transfers between devices, update(): lax.all_to_all(product.astype(jnp.bfloat16), 'axial', split_axis=1, conca...  17.1 us
    all_to_all x2, starting transfers between devices, channel_product(): lax.all_to_all(right_side, 'axial', split_axis=0, concat_axis=1, tiled=True)  10.9 us
    all_to_all x2, starting transfers between devices, update(): lax.all_to_all(product.astype(jnp.bfloat16), 'axial', split_axis=1, conca...  7.31 us
    all_to_all x2, starting transfers between devices, channel_product(): lax.all_to_all(left_side, 'axial', split_axis=0, concat_axis=1, tiled=True)  7.06 us
  transfers between devices with their start and end apart: 6, of which 6 were waited for; matrix products, arithmetic and copies ran while one was open for 3% of the time, Pallas kernels for 0%

commit v1 on v0

--- a/solution.py
+++ b/solution.py
@@ -1,6 +1,10 @@
+import functools
+
 import jax
 import jax.numpy as jnp
 from jax import lax
+from jax.experimental import pallas as pl
+from jax.experimental.pallas import tpu as pltpu
 from jax.sharding import PartitionSpec as P
 
 EPS = 1e-05
@@ -43,7 +47,299 @@
     return (pair_rep.astype(jnp.float32) + gating * result).astype(jnp.bfloat16)
 
 
-def on_device(
+MESH = pl.DeviceIdType.MESH
+CORES = 2
+SIDES = 2
+UP, DOWN, ACROSS, PEER = range(4)
+VMEM_BYTES = 56 * 1024 * 1024
+
+
+def fits(devices, pair_shape, proj_shape):
+    rows, tokens, channels = pair_shape
+    hidden = proj_shape[1] // 4
+    held = 2 * devices * rows * tokens * hidden * 2
+    work = 12 * rows * tokens * max(hidden, channels) * 4
+    return (
+        devices % (CORES * SIDES) == 0
+        and devices * rows == tokens
+        and rows <= 8
+        and tokens % 16 == 0
+        and channels == hidden
+        and hidden % 128 == 0
+        and held + work < VMEM_BYTES // 2
+    )
+
+
+def layer_norm(values, gain):
+    average = jnp.mean(values, axis=-1, keepdims=True)
+    centred = values - average
+    spread = jnp.mean(jnp.square(centred), axis=-1, keepdims=True)
+    return centred * lax.rsqrt(spread + EPS) * gain
+
+
+def dot(left, right):
+    return jnp.dot(left, right, preferred_element_type=jnp.float32)
+
+
+def gather_kernel(
+    devices,
+    pair_ref,
+    norm_out,
+    proj_out,
+    gate_out,
+    mid_out,
+    final_out,
+    norm_in,
+    proj_in,
+    gate_in,
+    mid_in,
+    final_in,
+    out_ref,
+    held,
+    columns_out,
+    columns_in,
+    columns_f32,
+    rows_f32,
+    left_f32,
+    tri,
+    gating,
+    normed_ref,
+    send_sem,
+    recv_sem,
+    columns_send_sem,
+    columns_recv_sem,
+):
+    rows, tokens, channels = pair_ref.shape
+    hidden = held.shape[-1]
+    pad = 8
+    length = devices // (CORES * SIDES)
+    me = lax.axis_index("axial")
+    core = me % CORES
+    side = (me // CORES) % SIDES
+    line = me // (CORES * SIDES)
+
+    def index(at, on, of):
+        return (at * SIDES + on) * CORES + of
+
+    def near(step):
+        if step == 0:
+            return line
+        low = jnp.minimum(line, length - 1 - line)
+        first = jnp.where(2 * line < length, 1, -1)
+        hop = (step + 1) // 2
+        both = line - first * hop if step % 2 else line + first * hop
+        alone = jnp.where(2 * line < length, step, length - 1 - step)
+        return jnp.where(step <= 2 * low, both, alone)
+
+    order = [near(step) for step in range(length)]
+    mine = [index(at, side, core) for at in order]
+    beside = [index(at, 1 - side, core) for at in order]
+    peers = [index(at, side, 1 - core) for at in order]
+    peers_beside = [index(at, 1 - side, 1 - core) for at in order]
+
+    targets = {
+        UP: index(jnp.minimum(line + 1, length - 1), side, core),
+        DOWN: index(jnp.maximum(line - 1, 0), side, core),
+        ACROSS: index(line, 1 - side, core),
+        PEER: index(line, side, 1 - core),
+    }
+
+    def copy(phase, way, block):
+        return pltpu.make_async_remote_copy(
+            src_ref=held.at[phase, block],
+            dst_ref=held.at[phase, block],
+            send_sem=send_sem.at[phase, way, block],
+            recv_sem=recv_sem.at[phase, block],
+            device_id={"axial": targets[way]},
+            device_id_type=MESH,
+        )
+
+    def along(phase, step, act):
+        at, block = order[step], mine[step]
+
+        @pl.when(jnp.logical_and(at <= line, line < length - 1))
+        def _():
+            act(copy(phase, UP, block))
+
+        @pl.when(jnp.logical_and(at >= line, line > 0))
+        def _():
+            act(copy(phase, DOWN, block))
+
+    def start(descriptor):
+        descriptor.start()
+
+    def finish_send(descriptor):
+        descriptor.wait_send()
+
+    def forward(phase, step):
+        along(phase, step, start)
+        copy(phase, ACROSS, mine[step]).start()
+        copy(phase, PEER, mine[step]).start()
+
+    def arrived(phase, block):
+        copy(phase, PEER, block).wait_recv()
+
+    def columns_copy(block, target):
+        return pltpu.make_async_remote_copy(
+            src_ref=columns_out.at[target],
+            dst_ref=columns_in.at[block],
+            send_sem=columns_send_sem.at[target],
+            recv_sem=columns_recv_sem.at[block],
+            device_id={"axial": target},
+            device_id_type=MESH,
+        )
+
+    def exchange(phase, multiply):
+        def from_line(step):
+            arrived(phase, mine[step])
+            forward(phase, step)
+
+        def from_side(step):
+            arrived(phase, beside[step])
+            copy(phase, PEER, beside[step]).start()
+
+        def from_peer(block):
+            arrived(phase, block)
+            multiply(block)
+
+        multiply(mine[0])
+        from_peer(peers[0])
+        for step in range(1, length + 1):
+            if step < length:
+                from_line(step)
+            from_side(step - 1)
+            if step < length:
+                multiply(mine[step])
+            multiply(beside[step - 1])
+            if step < length:
+                from_peer(peers[step])
+            from_peer(peers_beside[step - 1])
+
+    def finish_sends(phase):
+        for step in range(length):
+            along(phase, step, finish_send)
+            copy(phase, ACROSS, mine[step]).wait_send()
+            copy(phase, PEER, mine[step]).wait_send()
+            copy(phase, PEER, beside[step]).wait_send()
+
+    def split(values):
+        return values.reshape(rows, tokens, values.shape[-1])
+
+    def gated(projected):
+        return (jax.nn.sigmoid(projected[:, hidden:]) * projected[:, :hidden]).astype(jnp.bfloat16)
+
+    def outgoing_block(block):
+        def one(row, carry):
+            right = held[0, block, row].astype(jnp.float32)
+            total = jnp.sum(left_f32[...] * right[None], axis=1, keepdims=True)
+            tri[:, pl.ds(block * rows + row, 1), :] = total
+            return carry
+
+        lax.fori_loop(0, rows, one, 0)
+
+    def incoming_block(block):
+        @pl.when(block != me)
+        def _():
+            columns_copy(block, targets[PEER]).wait_recv()
+
+        rows_f32[...] = columns_in[block].astype(jnp.float32)
+
+        def one(tile, carry):
+            window = pl.ds(pl.multiple_of(tile * 16, 16), 16)
+            right = held[1, block, :, window, :].astype(jnp.float32)
+            for i in range(rows):
+                total = tri[i, window, :]
+                for l in range(rows):
+                    total = total + rows_f32[pl.ds(l * pad + i, 1), :] * right[l]
+                tri[i, window, :] = total
+            return carry
+
+        lax.fori_loop(0, tokens // 16, one, 0)
+
+    def close(pair, mid_gain, final):
+        product = tri[...].reshape(rows * tokens, hidden).astype(jnp.bfloat16).astype(jnp.float32)
+        normed = layer_norm(product, mid_gain[...]).astype(jnp.bfloat16)
+        return (pair + gating[...] * dot(normed, final[...])).astype(jnp.bfloat16)
+
+    barrier = pltpu.get_barrier_semaphore()
+    for offset in range(1, devices):
+        pl.semaphore_signal(
+            barrier,
+            inc=1,
+            device_id={"axial": lax.rem(me + offset, devices)},
+            device_id_type=MESH,
+        )
+
+    pair = pair_ref[...].astype(jnp.float32).reshape(rows * tokens, channels)
+    normed_ref[...] = layer_norm(pair, norm_out[...]).astype(jnp.bfloat16)
+    held[0, me] = split(gated(dot(normed_ref[...], proj_out[:, 2 * hidden :])))
+    pl.semaphore_wait(barrier, devices - 1)
+    forward(0, 0)
+    left_f32[...] = split(gated(dot(normed_ref[...], proj_out[:, : 2 * hidden]))).astype(jnp.float32)
+    gating[...] = jax.nn.sigmoid(dot(normed_ref[...], gate_out[...]))
+    exchange(0, outgoing_block)
+    first = close(pair, mid_out, final_out).astype(jnp.float32)
+    out_ref[...] = split(first).astype(jnp.bfloat16)
+
+    normed_ref[...] = layer_norm(first, norm_in[...]).astype(jnp.bfloat16)
+    held[1, me] = split(gated(dot(normed_ref[...], proj_in[:, 2 * hidden :])))
+    forward(1, 0)
+    left_f32[...] = split(gated(dot(normed_ref[...], proj_in[:, : 2 * hidden]))).astype(jnp.float32)
+    columns_f32[...] = jnp.zeros_like(columns_f32)
+    for target in range(devices):
+        for l in range(rows):
+            columns_f32[target, l * pad : l * pad + rows, :] = left_f32[
+                l, target * rows : (target + 1) * rows, :
+            ]
+    columns_out[...] = columns_f32[...].astype(jnp.bfloat16)
+    for offset in range(1, devices):
+        columns_copy(me, lax.rem(me + offset, devices)).start()
+    columns_in[me] = columns_out[me]
+    gating[...] = jax.nn.sigmoid(dot(normed_ref[...], gate_in[...]))
+    tri[...] = jnp.zeros_like(tri)
+    exchange(1, incoming_block)
+    again = out_ref[...].astype(jnp.float32).reshape(rows * tokens, channels)
+    out_ref[...] = split(close(again, mid_in, final_in))
+
+    for offset in range(1, devices):
+        columns_copy(me, lax.rem(me + offset, devices)).wait_send()
+    finish_sends(0)
+    finish_sends(1)
+
+
+def gather_rows(devices, pair_rep, *weights):
+    rows, tokens, channels = pair_rep.shape
+    hidden = weights[1].shape[1] // 4
+    gains = [w.reshape(1, -1) if w.ndim == 1 else w for w in weights]
+    packed = rows * 8
+    return pl.pallas_call(
+        functools.partial(gather_kernel, devices),
+        out_shape=jax.ShapeDtypeStruct(pair_rep.shape, pair_rep.dtype),
+        in_specs=[pl.BlockSpec(memory_space=pltpu.VMEM)] * 11,
+        out_specs=pl.BlockSpec(memory_space=pltpu.VMEM),
+        scratch_shapes=[
+            pltpu.VMEM((2, devices, rows, tokens, hidden), jnp.bfloat16),
+            pltpu.VMEM((devices, packed, hidden), jnp.bfloat16),
+            pltpu.VMEM((devices, packed, hidden), jnp.bfloat16),
+            pltpu.VMEM((devices, packed, hidden), jnp.float32),
+            pltpu.VMEM((packed, hidden), jnp.float32),
+            pltpu.VMEM((rows, tokens, hidden), jnp.float32),
+            pltpu.VMEM((rows, tokens, hidden), jnp.float32),
+            pltpu.VMEM((rows * tokens, channels), jnp.float32),
+            pltpu.VMEM((rows * tokens, channels), jnp.bfloat16),
+            pltpu.SemaphoreType.DMA((2, 4, devices)),
+            pltpu.SemaphoreType.DMA((2, devices)),
+            pltpu.SemaphoreType.DMA((devices,)),
+            pltpu.SemaphoreType.DMA((devices,)),
+        ],
+        compiler_params=pltpu.CompilerParams(
+            collective_id=0, has_side_effects=True, vmem_limit_bytes=VMEM_BYTES
+        ),
+        name="gather_rows",
+    )(pair_rep, *gains)
+
+
+def exchange_channels(
     pair_rep,
     norm_out,
     proj_out,
@@ -61,6 +357,13 @@
 
 
 def solution(mesh):
+    devices = mesh.shape["axial"]
+
+    def on_device(*arrays):
+        if fits(devices, arrays[0].shape, arrays[2].shape):
+            return gather_rows(devices, *arrays)
+        return exchange_channels(*arrays)
+
     placed = (P(("groups", "axial"), None, None), P(), P(), P(), P(), P(), P(), P(), P(), P(), P())
     return jax.shard_map(
         on_device,

time: 94.3 us -> 58.8 us (0.62)
  Pallas kernels: 0 us -> 56.5 us
  waiting for transfers between devices: 55.1 us -> 0 us
  starting transfers between devices: 25.3 us -> 0 us
  matrix products: 4.23 us -> 0 us
  local copies, waits for them, and re-layouts: 5.17 us -> 1.58 us
  other arithmetic: 3.23 us -> 0 us
    pallas_call x0 -> x1, Pallas kernels: none -> 56.5 us  [gather_rows(): pl.pallas_call(functools.partial(gather_kernel, devices), out_shape=jax.S...]
    all_to_all x6 -> x0, waiting for transfers between devices: 55.1 us -> none  [the longest x2 19.1 us: channel_product(): lax.all_to_all(right_side, 'axial', split_axis=0, concat_axis=1, tiled=True)]
    all_to_all x6 -> x0, starting transfers between devices: 25.3 us -> none  [the longest x2 10.9 us: channel_product(): lax.all_to_all(right_side, 'axial', split_axis=0, concat_axis=1, tiled=True)]
    convert_element_type x6 -> x0, local copies, waits for them, and re-layouts: 5 us -> none  [the longest x2 1.77 us: update(): (jax.nn.sigmoid(projected[hidden:2 * hidden]) * projected[:hidden]).astyp...]
    dot_general x8 -> x0, matrix products: 4.23 us -> none  [the longest x2 1.64 us: update(): jnp.einsum('rnc,ck->krn', normed, weights, preferred_element_type=jnp.flo...]
    reduce_sum x7 -> x0, other arithmetic: 2.85 us -> none  [the longest x4 1.66 us: normalize(): spread = jnp.mean(jnp.square(values - average), axis=axis, keepdims=True)]
    unnamed x22 -> x1, local copies, waits for them, and re-layouts: 0.06 us -> 1.58 us
  transfers between devices with their start and end apart: 6 -> 0, of which waited for: 6 -> 0; matrix products, arithmetic and copies ran while one was open for 3% -> 0% of each run, Pallas kernels for 0% -> 0%
where the time goes in v1:
time: 58.8 us; the launch traced here: 58.1 us
  Pallas kernels  56.5 us (96%)
  local copies, waits for them, and re-layouts  1.58 us (3%)
    pallas_call x1, Pallas kernels, gather_rows(): pl.pallas_call(functools.partial(gather_kernel, devices), out_shape=jax.S...  56.5 us
    unnamed x1, local copies, waits for them, and re-layouts  1.58 us

profile of v1, /device:TPU:0, one launch (start us, length us, event | category | flops | bytes accessed | tf_op | source)
XLA Modules:
  0.0 58.1 jit_solution(10007232438450186983)
XLA Ops:
  0.0 56.5 %gather_rows.1 = bf16[6,96,128]{2,1,0:T(8,128)(2,1)} custom-call(bf16[6,96,128]{2,1,0:T(8,128)(2,1)} %pair_ref.1, f32[1,128]{1,0:T(1,128)} %bitcast.4, bf16[128,512]{1,0:T(8,128)(2,1)} %proj_out.1, bf16[128,128]{1,0:T(8,128)(2,1)} %gate_out.1, f32[1,128]{1,0:T(1,128)} %bitcast.5, bf16[128,128]{1,0:T(8,128)(2,1)} %final_out.1, f32[1,128]{1,0:T(1,128)} %bitcast.6, ...), custom_call_target="tpu_custom_call" | custom-call | tf_op jit(solution)/shard_map/gather_rows/pallas_call | solution.py:315
  56.5 1.6 %copy.13 = bf16[6,96,128]{2,1,0:T(8,128)(2,1)} copy(bf16[6,96,128]{2,1,0:T(8,128)(2,1)} %gather_rows.1) | data formatting | bytes 294912

commit v2 on v1

v2 whole, which is shorter than its diff:
```python
import functools

import jax
import jax.numpy as jnp
from jax import lax
from jax.experimental import pallas as pl
from jax.experimental.pallas import tpu as pltpu
from jax.sharding import PartitionSpec as P

EPS = 1e-05


def normalize(values, gain, axis):
    average = jnp.mean(values, axis=axis, keepdims=True)
    spread = jnp.mean(jnp.square(values - average), axis=axis, keepdims=True)
    return (values - average) * lax.rsqrt(spread + EPS) * gain


def channel_product(left_side, right_side, outgoing):
    formula = "kil,kjl->kij" if outgoing else "kli,klj->kij"
    got_left, got_right = (
        lax.all_to_all(left_side, "axial", split_axis=0, concat_axis=1, tiled=True),
        lax.all_to_all(right_side, "axial", split_axis=0, concat_axis=1, tiled=True),
    )
    return jnp.einsum(formula, got_left, got_right, preferred_element_type=jnp.float32)


def update(pair_rep, norm_gain, weights, gate_weight, mid_gain, final_weight, outgoing):
    normed = normalize(pair_rep.astype(jnp.float32), norm_gain, -1).astype(jnp.bfloat16)
    projected = jnp.einsum("rnc,ck->krn", normed, weights, preferred_element_type=jnp.float32)
    hidden = weights.shape[1] // 4
    left_side = (jax.nn.sigmoid(projected[hidden : 2 * hidden]) * projected[:hidden]).astype(
        jnp.bfloat16
    )
    right_side = (
        jax.nn.sigmoid(projected[3 * hidden :]) * projected[2 * hidden : 3 * hidden]
    ).astype(jnp.bfloat16)
    product = channel_product(left_side, right_side, outgoing)
    tri = lax.all_to_all(
        product.astype(jnp.bfloat16), "axial", split_axis=1, concat_axis=0, tiled=True
    )
    gating = jax.nn.sigmoid(
        jnp.einsum("rnc,ce->rne", normed, gate_weight, preferred_element_type=jnp.float32)
    )
    tri_normed = normalize(tri.astype(jnp.float32), mid_gain[:, None, None], 0).astype(jnp.bfloat16)
    result = jnp.einsum("krn,kc->rnc", tri_normed, final_weight, preferred_element_type=jnp.float32)
    return (pair_rep.astype(jnp.float32) + gating * result).astype(jnp.bfloat16)


MESH = pl.DeviceIdType.MESH
CORES = 2
SIDES = 2
UP, DOWN, ACROSS = range(3)
VMEM_BYTES = 56 * 1024 * 1024


def fits(devices, pair_shape, proj_shape):
    rows, tokens, channels = pair_shape
    hidden = proj_shape[1] // 4
    held = 2 * devices * rows * tokens * hidden * 2
    work = 12 * rows * tokens * max(hidden, channels) * 4
    return (
        devices % (CORES * SIDES) == 0
        and devices * rows == tokens
        and rows <= 8
        and tokens % (16 * CORES) == 0
        and channels == hidden
        and hidden % 128 == 0
        and held + work < VMEM_BYTES // 2
    )


def layer_norm(values, gain):
    average = jnp.mean(values, axis=-1, keepdims=True)
    centred = values - average
    spread = jnp.mean(jnp.square(centred), axis=-1, keepdims=True)
    return centred * lax.rsqrt(spread + EPS) * gain


def dot(left, right):
    return jnp.dot(left, right, preferred_element_type=jnp.float32)


def gather_kernel(
    devices,
    pieces,
    pair_ref,
    norm_out,
    proj_out,
    gate_out,
    mid_out,
    final_out,
    norm_in,
    proj_in,
    gate_in,
    mid_in,
    final_in,
    out_ref,
    held,
    columns_out,
    columns_in,
    columns_f32,
    rows_f32,
    left_out,
    left_in,
    left_f32,
    partial,
    tri,
    part_out,
    part_in,
    gating,
    normed_ref,
    send_sem,
    recv_sem,
    columns_send_sem,
    columns_recv_sem,
    peer_send_sem,
    peer_recv_sem,
):
    rows, tokens, channels = pair_ref.shape
    hidden = held.shape[-1]
    chips = devices // CORES
    length = chips // SIDES
    both = CORES * rows
    pad = columns_out.shape[1] // rows
    share = chips * rows
    piece = rows // pieces
    me = lax.axis_index("axial")
    core = me % CORES
    chip = me // CORES
    side = chip % SIDES
    line = chip // SIDES
    low = jnp.minimum(line, length - 1 - line)

    def near(step):
        if step == 0:
            return line
        first = jnp.where(2 * line < length, 1, -1)
        hop = (step + 1) // 2
        pair = line - first * hop if step % 2 else line + first * hop
        alone = jnp.where(2 * line < length, step, length - 1 - step)
        return jnp.where(step <= 2 * low, pair, alone)

    def index(chip_at):
        return chip_at * CORES + core

    order = [near(step) for step in range(length)]
    mine = [at * SIDES + side for at in order]
    beside = [at * SIDES + 1 - side for at in order]
    peer = chip * CORES + 1 - core
    targets = {
        UP: index(jnp.minimum(line + 1, length - 1) * SIDES + side),
        DOWN: index(jnp.maximum(line - 1, 0) * SIDES + side),
        ACROSS: index(line * SIDES + 1 - side),
    }

    def line_event(event):
        step, part = 1 + event // pieces, event % pieces
        at = order[step]
        if event < 2 * pieces and length > 2:
            inner = low >= 1
            at = jnp.where(inner, order[1 + event % 2], at)
            part = jnp.where(inner, event // 2, part)
        return at, part

    def copy(phase, way, block, part):
        window = pl.ds(part * piece, piece)
        return pltpu.make_async_remote_copy(
            src_ref=held.at[phase, block, window],
            dst_ref=held.at[phase, block, window],
            send_sem=send_sem.at[phase, way, block, part],
            recv_sem=recv_sem.at[phase, block, part],
            device_id={"axial": targets[way]},
            device_id_type=MESH,
        )

    def pass_on(phase, at, part, act):
        block = at * SIDES + side

        @pl.when(jnp.logical_and(at <= line, line < length - 1))
        def _():
            act(copy(phase, UP, block, part))

        @pl.when(jnp.logical_and(at >= line, line > 0))
        def _():
            act(copy(phase, DOWN, block, part))

        act(copy(phase, ACROSS, block, part))

    def start(descriptor):
        descriptor.start()

    def finish_send(descriptor):
        descriptor.wait_send()

    def arrived(phase, block, part):
        copy(phase, ACROSS, block, part).wait_recv()

    def columns_copy(block, target):
        return pltpu.make_async_remote_copy(
            src_ref=columns_out.at[target],
            dst_ref=columns_in.at[block],
            send_sem=columns_send_sem.at[target],
            recv_sem=columns_recv_sem.at[block],
            device_id={"axial": index(target)},
            device_id_type=MESH,
        )

    def peer_copy(source, target, which):
        return pltpu.make_async_remote_copy(
            src_ref=source,
            dst_ref=target,
            send_sem=peer_send_sem.at[which],
            recv_sem=peer_recv_sem.at[which],
            device_id={"axial": peer},
            device_id_type=MESH,
        )

    left_copy = peer_copy(left_out, left_in, 0)
    tri_copy = peer_copy(part_out.at[0, :, :share], part_in.at[0, :, :share], 1)
    sum_copy = peer_copy(part_out.at[1], part_in.at[1], 2)

    def exchange(phase, multiply):
        def from_line(step):
            for event in range((step - 1) * pieces, step * pieces):
                at, part = line_event(event)
                arrived(phase, at * SIDES + side, part)
                pass_on(phase, at, part, start)

        def from_side(step):
            for part in range(pieces):
                arrived(phase, beside[step], part)
            multiply(beside[step])

        multiply(mine[0])
        if length > 1:
            from_line(1)
        from_side(0)
        for step in range(2, length):
            from_line(step)
            multiply(mine[step - 1])
            from_side(step - 1)
        if length > 1:
            multiply(mine[length - 1])
            from_side(length - 1)

    def finish_sends(phase):
        for step in range(length):
            for part in range(pieces):
                pass_on(phase, order[step], part, finish_send)

    def split(values):
        return values.reshape(rows, tokens, values.shape[-1])

    def gated(projected):
        return (jax.nn.sigmoid(projected[:, hidden:]) * projected[:, :hidden]).astype(jnp.bfloat16)

    def outgoing_block(block):
        def one(row, carry):
            right = held[0, block, row].astype(jnp.float32)
            at = pl.ds(block * rows + row, 1)
            for half in range(CORES):
                total = jnp.sum(left_f32[half] * right[None], axis=1, keepdims=True)
                partial[half, :, at, :] = total
            return carry

        lax.fori_loop(0, rows, one, 0)

    def incoming_block(block):
        @pl.when(block != chip)
        def _():
            columns_copy(block, chip * 0 + beside[0]).wait_recv()

        rows_f32[...] = columns_in[block].astype(jnp.float32)

        def one(tile, carry):
            window = pl.ds(pl.multiple_of(tile * 16, 16), 16)
            right = held[1, block, :, window, :].astype(jnp.float32)
            for i in range(both):
                total = partial[i // rows, i % rows, window, :]
                for l in range(rows):
                    total = total + rows_f32[pl.ds(l * pad + i, 1), :] * right[l]
                partial[i // rows, i % rows, window, :] = total
            return carry

        lax.fori_loop(0, tokens // 16, one, 0)

    def close(pair, mid_gain, final):
        product = tri[...].reshape(rows * tokens, hidden).astype(jnp.bfloat16).astype(jnp.float32)
        normed = layer_norm(product, mid_gain[...]).astype(jnp.bfloat16)
        return (pair + gating[...] * dot(normed, final[...])).astype(jnp.bfloat16)

    barrier = pltpu.get_barrier_semaphore()
    for offset in range(1, chips):
        pl.semaphore_signal(
            barrier,
            inc=1,
            device_id={"axial": index(lax.rem(chip + offset, chips))},
            device_id_type=MESH,
        )
    pl.semaphore_signal(barrier, inc=1, device_id={"axial": peer}, device_id_type=MESH)

    pair = pair_ref[...].astype(jnp.float32).reshape(rows * tokens, channels)
    normed_ref[...] = layer_norm(pair, norm_out[...]).astype(jnp.bfloat16)
    held[0, chip] = split(gated(dot(normed_ref[...], proj_out[:, 2 * hidden :])))
    pl.semaphore_wait(barrier, chips)
    for part in range(pieces):
        pass_on(0, line, part, start)
    left_out[...] = split(gated(dot(normed_ref[...], proj_out[:, : 2 * hidden])))
    left_copy.start()
    left_f32[0] = left_out[...].astype(jnp.float32)
    gating[...] = jax.nn.sigmoid(dot(normed_ref[...], gate_out[...]))
    left_copy.wait_recv()
    left_f32[1] = left_in[...].astype(jnp.float32)
    exchange(0, outgoing_block)
    part_out[0, :, :share] = partial[1, :, :share].astype(jnp.bfloat16)
    tri_copy.start()
    tri_copy.wait_recv()
    partial[1, :, :share] = part_in[0, :, :share].astype(jnp.float32)
    for half in range(CORES):
        for block in range(chips):
            at = (block * CORES + half) * rows
            got = pl.ds(block * rows, rows)
            tri[:, at : at + rows, :] = jnp.where(
                core == half, partial[0, :, got, :], partial[1, :, got, :]
            )
    first = close(pair, mid_out, final_out).astype(jnp.float32)
    out_ref[...] = split(first).astype(jnp.bfloat16)

    normed_ref[...] = layer_norm(first, norm_in[...]).astype(jnp.bfloat16)
    held[1, chip] = split(gated(dot(normed_ref[...], proj_in[:, 2 * hidden :])))
    for part in range(pieces):
        pass_on(1, line, part, start)
    left_f32[0] = split(gated(dot(normed_ref[...], proj_in[:, : 2 * hidden]))).astype(jnp.float32)
    columns_f32[...] = jnp.zeros_like(columns_f32)
    for target in range(chips):
        for l in range(rows):
            columns_f32[target, l * pad : l * pad + both, :] = left_f32[
                0, l, target * both : (target + 1) * both, :
            ]
    columns_out[...] = columns_f32[...].astype(jnp.bfloat16)
    for offset in range(1, chips):
        columns_copy(chip, lax.rem(chip + offset, chips)).start()
    columns_in[chip] = columns_out[chip]
    gating[...] = jax.nn.sigmoid(dot(normed_ref[...], gate_in[...]))
    partial[...] = jnp.zeros_like(partial)
    exchange(1, incoming_block)
    part_out[1] = partial[1 - core].astype(jnp.bfloat16)
    sum_copy.start()
    sum_copy.wait_recv()
    tri[...] = partial[core] + part_in[1].astype(jnp.float32)
    again = out_ref[...].astype(jnp.float32).reshape(rows * tokens, channels)
    out_ref[...] = split(close(again, mid_in, final_in))

    for offset in range(1, chips):
        columns_copy(chip, lax.rem(chip + offset, chips)).wait_send()
    left_copy.wait_send()
    tri_copy.wait_send()
    sum_copy.wait_send()
    finish_sends(0)
    finish_sends(1)


def gather_rows(devices, pair_rep, *weights):
    rows, tokens, channels = pair_rep.shape
    hidden = weights[1].shape[1] // 4
    gains = [w.reshape(1, -1) if w.ndim == 1 else w for w in weights]
    chips = devices // CORES
    packed = rows * (-(-CORES * rows // 8) * 8)
    pieces = 2 if rows % 2 == 0 else 1
    block = (rows, tokens, hidden)
    return pl.pallas_call(
        functools.partial(gather_kernel, devices, pieces),
        out_shape=jax.ShapeDtypeStruct(pair_rep.shape, pair_rep.dtype),
        in_specs=[pl.BlockSpec(memory_space=pltpu.VMEM)] * 11,
        out_specs=pl.BlockSpec(memory_space=pltpu.VMEM),
        scratch_shapes=[
            pltpu.VMEM((2, chips) + block, jnp.bfloat16),
            pltpu.VMEM((chips, packed, hidden), jnp.bfloat16),
            pltpu.VMEM((chips, packed, hidden), jnp.bfloat16),
            pltpu.VMEM((chips, packed, hidden), jnp.float32),
            pltpu.VMEM((packed, hidden), jnp.float32),
            pltpu.VMEM(block, jnp.bfloat16),
            pltpu.VMEM(block, jnp.bfloat16),
            pltpu.VMEM((CORES,) + block, jnp.float32),
            pltpu.VMEM((CORES,) + block, jnp.float32),
            pltpu.VMEM(block, jnp.float32),
            pltpu.VMEM((2,) + block, jnp.bfloat16),
            pltpu.VMEM((2,) + block, jnp.bfloat16),
            pltpu.VMEM((rows * tokens, channels), jnp.float32),
            pltpu.VMEM((rows * tokens, channels), jnp.bfloat16),
            pltpu.SemaphoreType.DMA((2, 3, chips, pieces)),
            pltpu.SemaphoreType.DMA((2, chips, pieces)),
            pltpu.SemaphoreType.DMA((chips,)),
            pltpu.SemaphoreType.DMA((chips,)),
            pltpu.SemaphoreType.DMA((3,)),
            pltpu.SemaphoreType.DMA((3,)),
        ],
        compiler_params=pltpu.CompilerParams(
            collective_id=0, has_side_effects=True, vmem_limit_bytes=VMEM_BYTES
        ),
        name="gather_rows",
    )(pair_rep, *gains)


def exchange_channels(
    pair_rep,
    norm_out,
    proj_out,
    gate_out,
    mid_out,
    final_out,
    norm_in,
    proj_in,
    gate_in,
    mid_in,
    final_in,
):
    first = update(pair_rep, norm_out, proj_out, gate_out, mid_out, final_out, True)
    return update(first, norm_in, proj_in, gate_in, mid_in, final_in, False)


def solution(mesh):
    devices = mesh.shape["axial"]

    def on_device(*arrays):
        if fits(devices, arrays[0].shape, arrays[2].shape):
            return gather_rows(devices, *arrays)
        return exchange_channels(*arrays)

    placed = (P(("groups", "axial"), None, None), P(), P(), P(), P(), P(), P(), P(), P(), P(), P())
    return jax.shard_map(
        on_device,
        mesh=mesh,
        in_specs=placed,
        out_specs=P(("groups", "axial"), None, None),
        check_vma=False,
    )
```

time: 58.8 us -> 53.6 us (0.912)
  Pallas kernels: 56.5 us -> 51.5 us
    pallas_call x1, Pallas kernels: 56.5 us -> 51.5 us  [gather_rows(): pl.pallas_call(functools.partial(gather_kernel, devices, pieces), out_sha...]
where the time goes in v2:
time: 53.6 us; the launch traced here: 53.1 us
  Pallas kernels  51.5 us (96%)
  local copies, waits for them, and re-layouts  1.58 us (3%)
    pallas_call x1, Pallas kernels, gather_rows(): pl.pallas_call(functools.partial(gather_kernel, devices, pieces), out_sha...  51.5 us
    unnamed x1, local copies, waits for them, and re-layouts  1.58 us

profile of v2, /device:TPU:0, one launch (start us, length us, event | category | flops | bytes accessed | tf_op | source)
XLA Modules:
  0.0 53.1 jit_solution(17895909625686093240)
XLA Ops:
  0.0 51.5 %gather_rows.1 = bf16[6,96,128]{2,1,0:T(8,128)(2,1)} custom-call(bf16[6,96,128]{2,1,0:T(8,128)(2,1)} %pair_ref.1, f32[1,128]{1,0:T(1,128)} %bitcast.4, bf16[128,512]{1,0:T(8,128)(2,1)} %proj_out.1, bf16[128,128]{1,0:T(8,128)(2,1)} %gate_out.1, f32[1,128]{1,0:T(1,128)} %bitcast.5, bf16[128,128]{1,0:T(8,128)(2,1)} %final_out.1, f32[1,128]{1,0:T(1,128)} %bitcast.6, ...), custom_call_target="tpu_custom_call" | custom-call | tf_op jit(solution)/shard_map/gather_rows/pallas_call | solution.py:372
  51.5 1.6 %copy.13 = bf16[6,96,128]{2,1,0:T(8,128)(2,1)} copy(bf16[6,96,128]{2,1,0:T(8,128)(2,1)} %gather_rows.1) | data formatting | bytes 294912

commit v3 on v2

--- a/solution.py
+++ b/solution.py
@@ -233,16 +233,16 @@
             multiply(beside[step])
 
         multiply(mine[0])
-        if length > 1:
-            from_line(1)
-        from_side(0)
-        for step in range(2, length):
+        for step in range(1, length):
             from_line(step)
-            multiply(mine[step - 1])
-            from_side(step - 1)
-        if length > 1:
-            multiply(mine[length - 1])
-            from_side(length - 1)
+            if step == 2:
+                from_side(0)
+            if 2 <= step < length - 1:
+                multiply(mine[step - 1])
+        for step in range(max(1, length - 2), length):
+            multiply(mine[step])
+        for step in range(1 if length > 2 else 0, length):
+            from_side(step)
 
     def finish_sends(phase):
         for step in range(length):

time: 53.6 us -> 47.3 us (0.88)
  Pallas kernels: 51.5 us -> 45.2 us
    pallas_call x1, Pallas kernels: 51.5 us -> 45.2 us  [gather_rows(): pl.pallas_call(functools.partial(gather_kernel, devices, pieces), out_sha...]
where the time goes in v3:
time: 47.3 us; the launch traced here: 46.8 us
  Pallas kernels  45.2 us (96%)
  local copies, waits for them, and re-layouts  1.58 us (3%)
    pallas_call x1, Pallas kernels, gather_rows(): pl.pallas_call(functools.partial(gather_kernel, devices, pieces), out_sha...  45.2 us
    unnamed x1, local copies, waits for them, and re-layouts  1.58 us

profile of v3, /device:TPU:0, one launch (start us, length us, event | category | flops | bytes accessed | tf_op | source)
XLA Modules:
  0.0 46.8 jit_solution(5444829511710132602)
XLA Ops:
  0.0 45.2 %gather_rows.1 = bf16[6,96,128]{2,1,0:T(8,128)(2,1)} custom-call(bf16[6,96,128]{2,1,0:T(8,128)(2,1)} %pair_ref.1, f32[1,128]{1,0:T(1,128)} %bitcast.4, bf16[128,512]{1,0:T(8,128)(2,1)} %proj_out.1, bf16[128,128]{1,0:T(8,128)(2,1)} %gate_out.1, f32[1,128]{1,0:T(1,128)} %bitcast.5, bf16[128,128]{1,0:T(8,128)(2,1)} %final_out.1, f32[1,128]{1,0:T(1,128)} %bitcast.6, ...), custom_call_target="tpu_custom_call" | custom-call | tf_op jit(solution)/shard_map/gather_rows/pallas_call | solution.py:372
  45.2 1.6 %copy.13 = bf16[6,96,128]{2,1,0:T(8,128)(2,1)} copy(bf16[6,96,128]{2,1,0:T(8,128)(2,1)} %gather_rows.1) | data formatting | bytes 294912

commit v4 on v3

--- a/solution.py
+++ b/solution.py
@@ -122,7 +122,7 @@
     chips = devices // CORES
     length = chips // SIDES
     both = CORES * rows
-    pad = columns_out.shape[1] // rows
+    pad = both
     share = chips * rows
     piece = rows // pieces
     me = lax.axis_index("axial")
@@ -285,10 +285,25 @@
 
         lax.fori_loop(0, tokens // 16, one, 0)
 
-    def close(pair, mid_gain, final):
-        product = tri[...].reshape(rows * tokens, hidden).astype(jnp.bfloat16).astype(jnp.float32)
+    def flat(values):
+        return values.reshape(-1, values.shape[-1])
+
+    def close(pair, part, mid_gain, final):
+        product = flat(tri[span(part)]).astype(jnp.bfloat16).astype(jnp.float32)
         normed = layer_norm(product, mid_gain[...]).astype(jnp.bfloat16)
-        return (pair + gating[...] * dot(normed, final[...])).astype(jnp.bfloat16)
+        return (pair + gating[flat_span(part)] * dot(normed, final[...])).astype(jnp.bfloat16)
+
+    def span(part):
+        return pl.ds(part * piece, piece)
+
+    def flat_span(part):
+        return pl.ds(part * piece * tokens, piece * tokens)
+
+    def open_piece(phase, part, pair, norm, proj):
+        normed = layer_norm(pair, norm[...]).astype(jnp.bfloat16)
+        normed_ref[flat_span(part)] = normed
+        right = gated(dot(normed, proj[:, 2 * hidden :]))
+        held[phase, chip, span(part)] = right.reshape(piece, tokens, hidden)
 
     barrier = pltpu.get_barrier_semaphore()
     for offset in range(1, chips):
@@ -300,11 +315,11 @@
         )
     pl.semaphore_signal(barrier, inc=1, device_id={"axial": peer}, device_id_type=MESH)
 
-    pair = pair_ref[...].astype(jnp.float32).reshape(rows * tokens, channels)
-    normed_ref[...] = layer_norm(pair, norm_out[...]).astype(jnp.bfloat16)
-    held[0, chip] = split(gated(dot(normed_ref[...], proj_out[:, 2 * hidden :])))
-    pl.semaphore_wait(barrier, chips)
     for part in range(pieces):
+        pair = flat(pair_ref[span(part)]).astype(jnp.float32)
+        open_piece(0, part, pair, norm_out, proj_out)
+        if part == 0:
+            pl.semaphore_wait(barrier, chips)
         pass_on(0, line, part, start)
     left_out[...] = split(gated(dot(normed_ref[...], proj_out[:, : 2 * hidden])))
     left_copy.start()
@@ -324,12 +339,11 @@
             tri[:, at : at + rows, :] = jnp.where(
                 core == half, partial[0, :, got, :], partial[1, :, got, :]
             )
-    first = close(pair, mid_out, final_out).astype(jnp.float32)
-    out_ref[...] = split(first).astype(jnp.bfloat16)
-
-    normed_ref[...] = layer_norm(first, norm_in[...]).astype(jnp.bfloat16)
-    held[1, chip] = split(gated(dot(normed_ref[...], proj_in[:, 2 * hidden :])))
     for part in range(pieces):
+        pair = flat(pair_ref[span(part)]).astype(jnp.float32)
+        first = close(pair, part, mid_out, final_out)
+        out_ref[span(part)] = first.reshape(piece, tokens, channels)
+        open_piece(1, part, first.astype(jnp.float32), norm_in, proj_in)
         pass_on(1, line, part, start)
     left_f32[0] = split(gated(dot(normed_ref[...], proj_in[:, : 2 * hidden]))).astype(jnp.float32)
     columns_f32[...] = jnp.zeros_like(columns_f32)
@@ -349,8 +363,9 @@
     sum_copy.start()
     sum_copy.wait_recv()
     tri[...] = partial[core] + part_in[1].astype(jnp.float32)
-    again = out_ref[...].astype(jnp.float32).reshape(rows * tokens, channels)
-    out_ref[...] = split(close(again, mid_in, final_in))
+    for part in range(pieces):
+        again = flat(out_ref[span(part)]).astype(jnp.float32)
+        out_ref[span(part)] = close(again, part, mid_in, final_in).reshape(piece, tokens, channels)
 
     for offset in range(1, chips):
         columns_copy(chip, lax.rem(chip + offset, chips)).wait_send()
@@ -366,7 +381,7 @@
     hidden = weights[1].shape[1] // 4
     gains = [w.reshape(1, -1) if w.ndim == 1 else w for w in weights]
     chips = devices // CORES
-    packed = rows * (-(-CORES * rows // 8) * 8)
+    packed = -(-CORES * rows * rows // 16) * 16
     pieces = 2 if rows % 2 == 0 else 1
     block = (rows, tokens, hidden)
     return pl.pallas_call(

time: 47.3 us -> 46.4 us (0.981)
  Pallas kernels: 45.2 us -> 44.4 us
    pallas_call x1, Pallas kernels: 45.2 us -> 44.4 us  [gather_rows(): pl.pallas_call(functools.partial(gather_kernel, devices, pieces), out_sha...]
where the time goes in v4:
time: 46.4 us; the launch traced here: 46 us
  Pallas kernels  44.4 us (96%)
  local copies, waits for them, and re-layouts  1.58 us (3%)
    pallas_call x1, Pallas kernels, gather_rows(): pl.pallas_call(functools.partial(gather_kernel, devices, pieces), out_sha...  44.4 us
    unnamed x1, local copies, waits for them, and re-layouts  1.58 us

profile of v4, /device:TPU:0, one launch (start us, length us, event | category | flops | bytes accessed | tf_op | source)
XLA Modules:
  0.0 46.0 jit_solution(11448460868968630115)
XLA Ops:
  0.0 44.4 %gather_rows.1 = bf16[6,96,128]{2,1,0:T(8,128)(2,1)} custom-call(bf16[6,96,128]{2,1,0:T(8,128)(2,1)} %pair_ref.1, f32[1,128]{1,0:T(1,128)} %bitcast.4, bf16[128,512]{1,0:T(8,128)(2,1)} %proj_out.1, bf16[128,128]{1,0:T(8,128)(2,1)} %gate_out.1, f32[1,128]{1,0:T(1,128)} %bitcast.5, bf16[128,128]{1,0:T(8,128)(2,1)} %final_out.1, f32[1,128]{1,0:T(1,128)} %bitcast.6, ...), custom_call_target="tpu_custom_call" | custom-call | tf_op jit(solution)/shard_map/gather_rows/pallas_call | solution.py:387
  44.4 1.6 %copy.13 = bf16[6,96,128]{2,1,0:T(8,128)(2,1)} copy(bf16[6,96,128]{2,1,0:T(8,128)(2,1)} %gather_rows.1) | data formatting | bytes 294912

commit v5 on v4

--- a/solution.py
+++ b/solution.py
@@ -382,7 +382,7 @@
     gains = [w.reshape(1, -1) if w.ndim == 1 else w for w in weights]
     chips = devices // CORES
     packed = -(-CORES * rows * rows // 16) * 16
-    pieces = 2 if rows % 2 == 0 else 1
+    pieces = next(count for count in (3, 2, 1) if rows % count == 0)
     block = (rows, tokens, hidden)
     return pl.pallas_call(
         functools.partial(gather_kernel, devices, pieces),

time: 46.4 us -> 46.1 us (level)
  no operation moved by 1% of the time
where the time goes in v5:
time: 46.1 us; the launch traced here: 45.7 us
  Pallas kernels  44.1 us (96%)
  local copies, waits for them, and re-layouts  1.58 us (3%)
    pallas_call x1, Pallas kernels, gather_rows(): pl.pallas_call(functools.partial(gather_kernel, devices, pieces), out_sha...  44.1 us
    unnamed x1, local copies, waits for them, and re-layouts  1.58 us

profile of v5, /device:TPU:0, one launch (start us, length us, event | category | flops | bytes accessed | tf_op | source)
XLA Modules:
  0.0 45.7 jit_solution(4849115211179453116)
XLA Ops:
  0.0 44.1 %gather_rows.1 = bf16[6,96,128]{2,1,0:T(8,128)(2,1)} custom-call(bf16[6,96,128]{2,1,0:T(8,128)(2,1)} %pair_ref.1, f32[1,128]{1,0:T(1,128)} %bitcast.4, bf16[128,512]{1,0:T(8,128)(2,1)} %proj_out.1, bf16[128,128]{1,0:T(8,128)(2,1)} %gate_out.1, f32[1,128]{1,0:T(1,128)} %bitcast.5, bf16[128,128]{1,0:T(8,128)(2,1)} %final_out.1, f32[1,128]{1,0:T(1,128)} %bitcast.6, ...), custom_call_target="tpu_custom_call" | custom-call | tf_op jit(solution)/shard_map/gather_rows/pallas_call | solution.py:387
  44.1 1.6 %copy.13 = bf16[6,96,128]{2,1,0:T(8,128)(2,1)} copy(bf16[6,96,128]{2,1,0:T(8,128)(2,1)} %gather_rows.1) | data formatting | bytes 294912
